TPU v7x, 32 devices: a whole 2x2x4 slice. The times are simulated.
32 devices in a mesh: gx: 4 (over y, core), gy: 8 (over z, x).
Axes of the slice: x: 2, y: 2, z: 4, core: 2. Of those that a mesh axis runs over, the one named last changes fastest.
Arguments:
- previous: float32 [2, 7, 512, 1024], P(None, None, 'gx', 'gy'), may hold values from -6 to 6
- dissipated: float32 [2, 4, 512, 1024], P(None, None, 'gx', 'gy'), may hold values from 0.05 to 3
- material: int32 [4, 512, 1024], P(None, 'gx', 'gy'), may hold values from 0 to 3
- coolant: int32 [3, 512, 1024], P(None, 'gx', 'gy'), may hold values from 0 to 3
Outputs:
- temperature: float32 [2, 7, 512, 1024], P(None, None, 'gx', 'gy')
All inputs are finite; a program needn't handle non-finite values.
Results may differ from a plain program's by a relative error of at most 0.00011.
Values sent between devices are 32-bit elements; how exact they have to be, the bound alone decides.
A program may use at most 64 MiB of HBM per device.

v0:
```python
import jax
import jax.numpy as jnp
from jax import lax
from jax.sharding import PartitionSpec as P

ITERS = 3


TIER_K = (1.0, 0.3, 0.12, 2.5)
CHANNEL_K = (1.0, 0.3, 0.25, 0.2)
CHANNEL_SINK = (0.0, 0.15, 0.45, 1.2)
TIER_HEAT = 0.05
CHANNEL_HEAT = 0.2
VERTICAL = 4.0


def extended_2(x, sides, width):
    for axis, dim in sides:
        devices, length = (lax.axis_size(axis), x.shape[dim])
        up = [(i, (i + 1) % devices) for i in range(devices - 1)]
        down = [(j, i) for i, j in up]
        last = lax.slice_in_dim(x, length - width, length, axis=dim)
        leading = lax.slice_in_dim(x, 0, width, axis=dim)
        before = lax.ppermute(last, axis, up)
        after = lax.ppermute(leading, axis, down)
        x = jnp.concatenate([before, x, after], axis=dim)
    return x


def lookup(codes, table):
    total = jnp.zeros(codes.shape, jnp.float32)
    for index, value in enumerate(table):
        total = total + jnp.where(codes == index, jnp.float32(value), jnp.float32(0.0))
    return total


def mix(tiers, channels):
    rows = []
    for layer in range(2 * tiers.shape[0] - 1):
        rows.append(tiers[layer // 2] if layer % 2 == 0 else channels[layer // 2])
    return jnp.stack(rows)


def spread_power(heat):
    tiers = heat.shape[1]
    empty = jnp.zeros_like(heat[:, 0])
    rows = []
    for layer in range(2 * tiers - 1):
        rows.append(heat[:, layer // 2] if layer % 2 == 0 else empty)
    return jnp.stack(rows, 1)


def capacity_column(layers):
    return jnp.array(
        [TIER_HEAT if layer % 2 == 0 else CHANNEL_HEAT for layer in range(layers)], jnp.float32
    )


def couplings(padded_k):
    centre = padded_k[:, 1:-1, 1:-1]
    g_north = jnp.sqrt(centre * padded_k[:, :-2, 1:-1])
    g_south = jnp.sqrt(centre * padded_k[:, 2:, 1:-1])
    g_west = jnp.sqrt(centre * padded_k[:, 1:-1, :-2])
    g_east = jnp.sqrt(centre * padded_k[:, 1:-1, 2:])
    g_vertical = VERTICAL * jnp.sqrt(centre[:-1] * centre[1:])
    return (g_north, g_south, g_west, g_east, g_vertical)


def operate(padded_v, padded_k, sink, capacity):
    g_north, g_south, g_west, g_east, g_vertical = couplings(padded_k)
    centre = padded_v[:, :, 1:-1, 1:-1]
    lateral = g_north * (centre - padded_v[:, :, :-2, 1:-1]) + g_south * (
        centre - padded_v[:, :, 2:, 1:-1]
    )
    lateral = (
        lateral
        + g_west * (centre - padded_v[:, :, 1:-1, :-2])
        + g_east * (centre - padded_v[:, :, 1:-1, 2:])
    )
    flux = g_vertical * (centre[:, :-1] - centre[:, 1:])
    zero_row = jnp.zeros_like(centre[:, :1])
    vertical = jnp.concatenate([flux, zero_row], 1) - jnp.concatenate([zero_row, flux], 1)
    return (capacity + sink) * centre + lateral + vertical


def diagonal_terms(padded_k, sink, capacity):
    g_north, g_south, g_west, g_east, g_vertical = couplings(padded_k)
    zero_row = jnp.zeros_like(g_vertical[:1])
    vertical = jnp.concatenate([g_vertical, zero_row], 0) + jnp.concatenate(
        [zero_row, g_vertical], 0
    )
    return capacity + sink + g_north + g_south + g_west + g_east + vertical


def core_sum(first, second):
    return jnp.sum(first * second, axis=(1, 2, 3))


def both_sums(residual, scaled, image):
    return lax.psum((core_sum(residual, scaled), core_sum(scaled, image)), ("gx", "gy"))


def per_device(previous, dissipated, material, coolant):
    tiers = material.shape[0]
    layers = 2 * tiers - 1
    capacity = capacity_column(layers)[:, None, None]
    tier_k = lookup(material, TIER_K)
    kappa = mix(tier_k, lookup(coolant, CHANNEL_K))
    channel_sink = lookup(coolant, CHANNEL_SINK)
    conductivity = extended_2(kappa, (("gx", 1), ("gy", 2)), 1)
    coolant_sink = mix(jnp.zeros_like(tier_k), channel_sink)
    margin_start = 0

    def apply_operator(field, margin):
        extended = extended_2(field, (("gx", 2), ("gy", 3)), 1)
        result = operate(extended, conductivity, coolant_sink, capacity)
        return (result, margin)

    diagonal = diagonal_terms(conductivity, coolant_sink, capacity)
    source = capacity * previous + spread_power(dissipated)
    image, margin = apply_operator(previous, margin_start)
    residual = source - image
    solution = previous
    scaled = residual / diagonal
    image, inner_margin = apply_operator(scaled, margin)
    energy, curvature_now = both_sums(residual, scaled, image)
    step_size = energy / curvature_now
    direction = scaled
    along = image
    margin = inner_margin
    for iteration in range(ITERS):
        solution = solution + step_size[:, None, None, None] * direction
        residual = residual - step_size[:, None, None, None] * along
        if iteration + 1 < ITERS:
            scaled = residual / diagonal
            image, inner_margin = apply_operator(scaled, margin)
            energy_next, curvature_now = both_sums(residual, scaled, image)
            growth = energy_next / energy
            step_size = energy_next / (curvature_now - growth * energy_next / step_size)
            factor = growth[:, None, None, None]
            direction = scaled + factor * direction
            along = image + factor * along
            margin = inner_margin
            energy = energy_next
    return solution


def solution(mesh):
    return jax.shard_map(
        per_device,
        mesh=mesh,
        in_specs=(
            P(None, None, "gx", "gy"),
            P(None, None, "gx", "gy"),
            P(None, "gx", "gy"),
            P(None, "gx", "gy"),
        ),
        out_specs=P(None, None, "gx", "gy"),
        check_vma=False,
    )
```

profile of v0, /device:TPU:0, one launch (start us, length us, event | category | flops | bytes accessed | tf_op | source)
XLA Modules:
  0.0 283.8 jit_solution(1892046935967206937)
XLA Ops:
  3.3 3.7 %collective-permute-start.1 = (f32[2,7,1,128]{3,1,2,0:T(8,128)}, f32[2,7,1,128]{3,1,2,0:T(8,128)}, u32[]{:S(2)}, u32[]{:S(2)}) collective-permute-start(f32[2,7,1,128]{3,1,2,0:T(8,128)} %copy.160), channel_id=1, source_target_pairs={{0,8},{8,16},{16,24},{1,9},{9,17},{17,25},{2,10},{10,18},{18,26},{... | collective-permute-start | bytes 21512 | tf_op jit(solution)/shard_map/ppermute | solution.py:24
  10.3 4.6 %collective-permute-start = (f32[7,1,128]{2,1,0:T(1,128)}, f32[7,1,128]{2,1,0:T(1,128)S(1)}, u32[]{:S(2)}, u32[]{:S(2)}) collective-permute-start(f32[7,1,128]{2,1,0:T(1,128)} %get-tuple-element.55), channel_id=1, source_target_pairs={{0,8},{8,16},{16,24},{1,9},{9,17},{17,25},{2,10},{10,18},{18,26},{... | collective-permute-start | bytes 10760 | tf_op jit(solution)/shard_map/ppermute | solution.py:24
  27.0 2.4 stack.15
  32.4 5.4 %collective-permute-start.4 = (f32[7,130,1]{2,1,0:T(8,128)}, f32[7,130,1]{2,1,0:T(8,128)}, u32[]{:S(2)}, u32[]{:S(2)}) collective-permute-start(f32[7,130,1]{2,1,0:T(8,128)} %get-tuple-element.52), channel_id=1, source_target_pairs={{0,1},{1,2},{2,3},{3,4},{4,5},{5,6},{6,7},{8,9},{9,10},{10,11},{11... | collective-permute-start | bytes 10928 | tf_op jit(solution)/shard_map/ppermute | solution.py:24
  40.3 3.6 %collective-permute-start.5 = (f32[2,7,130,1]{2,1,3,0:T(8,128)}, f32[2,7,130,1]{2,1,3,0:T(8,128)S(1)}, u32[]{:S(2)}, u32[]{:S(2)}) collective-permute-start(f32[2,7,130,1]{2,1,3,0:T(8,128)} %get-tuple-element.37), channel_id=1, source_target_pairs={{0,1},{1,2},{2,3},{3,4},{4,5},{5,6},{6,7},{8,9},{9,10},{10,11},{11... | collective-permute-start | bytes 21848 | tf_op jit(solution)/shard_map/ppermute | solution.py:24
  46.6 11.4 %collective-permute-done.4 = f32[7,130,1]{2,1,0:T(8,128)} collective-permute-done((f32[7,130,1]{2,1,0:T(8,128)}, f32[7,130,1]{2,1,0:T(8,128)}, u32[]{:S(2)}, u32[]{:S(2)}) %collective-permute-start.4) | collective-permute-done | bytes 3672 | tf_op jit(solution)/shard_map/ppermute | solution.py:24
  58.0 3.0 %add_add_fusion = (f32[7,128,128]{2,1,0:T(8,128)}, f32[7,128,128]{2,1,0:T(8,128)}, f32[7,128,128]{2,1,0:T(8,128)S(1)}, f32[7,128,128]{2,1,0:T(8,128)S(1)}, f32[7...) fusion(f32[6,128,128]{2,1,0:T(8,128)S(1)} %sqrt_multiply_fusion, f32[7,128,128]{2,1,0:T(8,128)S(1)} %copy-done.33, ...), kind=kLoop, calls=%fused_computation.123 | loop fusion | flops 2179072 | bytes 4077708 | tf_op jit(solution)/shard_map/add | solution.py:92
  61.0 2.1 copy.139
  68.2 5.3 %broadcast_divide_fusion.2 = (f32[2,7,128,128]{2,1,3,0:T(8,128)S(1)}, f32[2,7,128,128]{2,1,3,0:T(8,128)S(1)}) fusion(f32[7,128,128]{1,0,2:T(8,128)} %copy.139, f32[2,6,128,128]{2,1,3,0:T(8,128)} %fusion.44, f32[2,7,128,128]{2,1,3,0:T(8,128)S(1)} %copy.146, f32[2,7,130,1]{2,1,3,0:T(8,128)} %collective-permute-done.7, f32[2,7,1,128]{2,1,3,0:T(8,128)} %copy-done.26, ...), kind=kLoop, calls=%fused_computation.105 | loop fusion | flops 6193152 | bytes 7237884 | tf_op jit(solution)/shard_map/div | solution.py:124
  76.5 2.1 collective-permute-start.8
  84.4 4.3 %collective-permute-start.10 = (f32[2,7,130,1]{2,1,3,0:T(8,128)S(1)}, f32[2,7,130,1]{2,1,3,0:T(8,128)S(1)}, u32[]{:S(2)}, u32[]{:S(2)}) collective-permute-start(f32[2,7,130,1]{2,1,3,0:T(8,128)S(1)} %get-tuple-element.35), channel_id=1, source_target_pairs={{0,1},{1,2},{2,3},{3,4},{4,5},{5,6},{6,7},{8,9},{9,10},{10,11},{11... | collective-permute-start | bytes 21848 | tf_op jit(solution)/shard_map/ppermute | solution.py:24
  90.5 4.2 %collective-permute-done.11 = f32[2,7,130,1]{2,1,3,0:T(8,128)S(1)} collective-permute-done((f32[2,7,130,1]{2,1,3,0:T(8,128)S(1)}, f32[2,7,130,1]{2,1,3,0:T(8,128)S(1)}, u32[]{:S(2)}, u32[]{:S(2)}) %collective-permute-start.11) | collective-permute-done | bytes 7312 | tf_op jit(solution)/shard_map/ppermute | solution.py:25
  94.7 3.0 %multiply_reduce_fusion.3 = (f32[2]{0:T(128)S(1)}, f32[2]{0:T(128)S(1)}, f32[2,7,128,128]{2,1,3,0:T(8,128)}) fusion(f32[2,7,128,128]{2,1,3,0:T(8,128)S(1)} %get-tuple-element.24, f32[2,7,128,128]{2,1,3,0:T(8,128)S(1)} %get-tuple-element.25, f32[2,6,128,128]{2,1,3,0:T(8,128)S(1)} %fusion.30, f32[2,7,130,1]{2,1,3,0:T(8,128)S(1)} %collective-permute-done.11, ...), kind=kLoop, calls=%fused_computation.101 | loop fusion | flops 6193148 | bytes 5861616 | tf_op jit(solution)/shard_map/reduce_sum | solution.py:96
  97.7 40.7 %all-reduce.12 = (f32[2]{0:T(128)S(1)}, f32[2]{0:T(128)S(1)}) all-reduce(f32[2]{0:T(128)S(1)} %get-tuple-element.8, f32[2]{0:T(128)S(1)} %get-tuple-element.7), channel_id=1, replica_groups=mesh['gx'=4,'gy'=8] {'gx','gy'}, use_global_device_ids=true, to_apply=%region_1.2 | all-reduce | flops 4 | bytes 32 | tf_op jit(solution)/shard_map/psum | solution.py:100
  138.5 1.6 broadcast_divide_fusion.1
  140.1 1.7 fusion.76
  149.0 2.7 collective-permute-done.13
  154.1 2.5 collective-permute-start.14
  156.6 1.6 collective-permute-start.15
  158.3 4.2 %collective-permute-done.15 = f32[2,7,130,1]{2,1,3,0:T(8,128)S(1)} collective-permute-done((f32[2,7,130,1]{2,1,3,0:T(8,128)S(1)}, f32[2,7,130,1]{2,1,3,0:T(8,128)S(1)}, u32[]{:S(2)}, u32[]{:S(2)}) %collective-permute-start.15) | collective-permute-done | bytes 7312 | tf_op jit(solution)/shard_map/ppermute | solution.py:25
  162.6 3.2 %multiply_reduce_fusion.1 = (f32[2]{0:T(128)S(1)}, f32[2]{0:T(128)S(1)}, f32[2,7,128,128]{2,1,3,0:T(8,128)}) fusion(f32[2,7,128,128]{2,1,3,0:T(8,128)S(1)} %broadcast_divide_fusion.1, f32[2,7,128,128]{2,1,3,0:T(8,128)S(1)} %get-tuple-element.25, f32[2,7,128,128]{2,1,3,0:T(8,128)S(1)} %copy-done.3, f32[2]{0:T(128)S(1)} %div.43, ...), kind=kLoop, calls=%fused_computation.98 | loop fusion | flops 6651900 | bytes 6779128 | tf_op jit(solution)/shard_map/reduce_sum | solution.py:96
  165.7 42.0 %all-reduce.11 = (f32[2]{0:T(128)S(1)}, f32[2]{0:T(128)S(1)}) all-reduce(f32[2]{0:T(128)S(1)} %get-tuple-element.6, f32[2]{0:T(128)S(1)} %get-tuple-element.5), channel_id=1, replica_groups=mesh['gx'=4,'gy'=8] {'gx','gy'}, use_global_device_ids=true, to_apply=%region_5.6 | all-reduce | flops 4 | bytes 32 | tf_op jit(solution)/shard_map/psum | solution.py:100
  207.7 3.4 %broadcast_divide_fusion = (f32[2,7,128,128]{2,1,3,0:T(8,128)S(1)}, f32[2,7,128,128]{2,1,3,0:T(8,128)}) fusion(f32[7,128,128]{1,0,2:T(8,128)} %copy.139, f32[2,7,128,128]{2,1,3,0:T(8,128)} %get-tuple-element.22, f32[2,7,128,128]{2,1,3,0:T(8,128)} %get-tuple-element.23, f32[2]{0:T(128)S(1)} %get-tuple-element.21, f32[2]{0:T(128)S(1)} %get-tuple-element.19, ...), kind=kLoop, calls=%fused_computation.103 | loop fusion | flops 1605632 | bytes 5046296 | tf_op jit(solution)/shard_map/div | solution.py:135
  211.1 1.7 fusion.75
  214.3 1.6 copy.155
  217.2 3.0 %collective-permute-start.16 = (f32[2,7,1,128]{3,1,2,0:T(8,128)S(1)}, f32[2,7,1,128]{3,1,2,0:T(8,128)S(1)}, u32[]{:S(2)}, u32[]{:S(2)}) collective-permute-start(f32[2,7,1,128]{3,1,2,0:T(8,128)S(1)} %copy.153), channel_id=1, source_target_pairs={{0,8},{8,16},{16,24},{1,9},{9,17},{17,25},{2,10},{10,18},{18,26},{... | collective-permute-start | bytes 21512 | tf_op jit(solution)/shard_map/ppermute | solution.py:24
  220.2 2.2 fusion
  226.1 4.2 %collective-permute-start.18 = (f32[2,7,130,1]{2,1,3,0:T(8,128)S(1)}, f32[2,7,130,1]{2,1,3,0:T(8,128)S(1)}, u32[]{:S(2)}, u32[]{:S(2)}) collective-permute-start(f32[2,7,130,1]{2,1,3,0:T(8,128)S(1)} %get-tuple-element.31), channel_id=1, source_target_pairs={{0,1},{1,2},{2,3},{3,4},{4,5},{5,6},{6,7},{8,9},{9,10},{10,11},{11... | collective-permute-start | bytes 21848 | tf_op jit(solution)/shard_map/ppermute | solution.py:24
  231.9 4.0 %collective-permute-done.19 = f32[2,7,130,1]{2,1,3,0:T(8,128)S(1)} collective-permute-done((f32[2,7,130,1]{2,1,3,0:T(8,128)S(1)}, f32[2,7,130,1]{2,1,3,0:T(8,128)S(1)}, u32[]{:S(2)}, u32[]{:S(2)}) %collective-permute-start.19) | collective-permute-done | bytes 7312 | tf_op jit(solution)/shard_map/ppermute | solution.py:25
  235.9 4.1 %fusion.7 = f32[2]{0:T(128)S(1)} fusion(f32[2,7,128,128]{2,1,3,0:T(8,128)S(1)} %get-tuple-element.17, f32[2,7,130,1]{2,1,3,0:T(8,128)S(1)} %collective-permute-done.19, f32[2,7,1,128]{2,1,3,0:T(8,128)} %copy.156, f32[2,7,1,128]{2,1,3,0:T(8,128)} %copy.154, f32[2,7,130,1]{2,1,3,0:T(8,128)S(1)} %collective-permute-done.18, f32[2,6,128,128]{2,1,3,0:T(8,128)} %fusion, ...), kind=kLoop, calls=%fused_computation.9 | loop fusion | flops 5734398 | bytes 4026600 | tf_op jit(solution)/shard_map/reduce_sum | solution.py:96
  240.0 40.4 %all-reduce.10 = (f32[2]{0:T(128)S(1)}, f32[2]{0:T(128)S(1)}) all-reduce(f32[2]{0:T(128)S(1)} %multiply_reduce_fusion, f32[2]{0:T(128)S(1)} %fusion.7), channel_id=1, replica_groups=mesh['gx'=4,'gy'=8] {'gx','gy'}, use_global_device_ids=true, to_apply=%region_9.10 | all-reduce | flops 4 | bytes 32 | tf_op jit(solution)/shard_map/psum | solution.py:100
  280.4 2.1 multiply_add_fusion
  (181 shorter events, 61.2 us)
Async XLA Ops:
  1.5 37.4 %collective-permute-start.3 = (f32[2,7,1,128]{3,1,2,0:T(8,128)}, f32[2,7,1,128]{3,1,2,0:T(8,128)S(1)}, u32[]{:S(2)}, u32[]{:S(2)}) collective-permute-start(f32[2,7,1,128]{3,1,2,0:T(8,128)} %copy.161), channel_id=1, source_target_pairs={{8,0},{16,8},{24,16},{9,1},{17,9},{25,17},{10,2},{18,10},{26,18},{... | collective-permute-start | bytes 21512 | tf_op jit(solution)/shard_map/ppermute | solution.py:25
  3.3 34.5 %collective-permute-start.1 = (f32[2,7,1,128]{3,1,2,0:T(8,128)}, f32[2,7,1,128]{3,1,2,0:T(8,128)}, u32[]{:S(2)}, u32[]{:S(2)}) collective-permute-start(f32[2,7,1,128]{3,1,2,0:T(8,128)} %copy.160), channel_id=1, source_target_pairs={{0,8},{8,16},{16,24},{1,9},{9,17},{17,25},{2,10},{10,18},{18,26},{... | collective-permute-start | bytes 21512 | tf_op jit(solution)/shard_map/ppermute | solution.py:24
  8.4 21.0 %copy-start.29 = (f32[7,128,128]{2,1,0:T(8,128)}, f32[7,128,128]{2,1,0:T(8,128)S(1)}, u32[]{:S(2)}) copy-start(f32[7,128,128]{2,1,0:T(8,128)S(1)} %get-tuple-element.56) | copy-start | bytes 1376260
  9.0 20.4 %collective-permute-start.2 = (f32[7,1,128]{2,1,0:T(1,128)}, f32[7,1,128]{2,1,0:T(1,128)S(1)}, u32[]{:S(2)}, u32[]{:S(2)}) collective-permute-start(f32[7,1,128]{2,1,0:T(1,128)} %get-tuple-element.54), channel_id=1, source_target_pairs={{8,0},{16,8},{24,16},{9,1},{17,9},{25,17},{10,2},{18,10},{26,18},{... | collective-permute-start | bytes 10760 | tf_op jit(solution)/shard_map/ppermute | solution.py:25
  10.3 19.1 %collective-permute-start = (f32[7,1,128]{2,1,0:T(1,128)}, f32[7,1,128]{2,1,0:T(1,128)S(1)}, u32[]{:S(2)}, u32[]{:S(2)}) collective-permute-start(f32[7,1,128]{2,1,0:T(1,128)} %get-tuple-element.55), channel_id=1, source_target_pairs={{0,8},{8,16},{16,24},{1,9},{9,17},{17,25},{2,10},{10,18},{18,26},{... | collective-permute-start | bytes 10760 | tf_op jit(solution)/shard_map/ppermute | solution.py:24
  15.9 52.3 %copy-start = (f32[2,7,128,128]{2,1,3,0:T(8,128)}, f32[2,7,128,128]{2,1,3,0:T(8,128)S(1)}, u32[]{:S(2)}) copy-start(f32[2,7,128,128]{2,1,3,0:T(8,128)S(1)} %copy.146) | copy-start | bytes 2752516
  31.1 15.4 %collective-permute-start.6 = (f32[7,130,1]{2,1,0:T(8,128)}, f32[7,130,1]{2,1,0:T(8,128)}, u32[]{:S(2)}, u32[]{:S(2)}) collective-permute-start(f32[7,130,1]{2,1,0:T(8,128)} %get-tuple-element.51), channel_id=1, source_target_pairs={{1,0},{2,1},{3,2},{4,3},{5,4},{6,5},{7,6},{9,8},{10,9},{11,10},{12... | collective-permute-start | bytes 10928 | tf_op jit(solution)/shard_map/ppermute | solution.py:25
  32.4 25.6 %collective-permute-start.4 = (f32[7,130,1]{2,1,0:T(8,128)}, f32[7,130,1]{2,1,0:T(8,128)}, u32[]{:S(2)}, u32[]{:S(2)}) collective-permute-start(f32[7,130,1]{2,1,0:T(8,128)} %get-tuple-element.52), channel_id=1, source_target_pairs={{0,1},{1,2},{2,3},{3,4},{4,5},{5,6},{6,7},{8,9},{9,10},{10,11},{11... | collective-permute-start | bytes 10928 | tf_op jit(solution)/shard_map/ppermute | solution.py:24
  39.3 18.7 %copy-start.30 = (f32[7,128,128]{2,1,0:T(8,128)S(1)}, f32[7,128,128]{2,1,0:T(8,128)}, u32[]{:S(2)}) copy-start(f32[7,128,128]{2,1,0:T(8,128)} %copy-done.29) | copy-start | bytes 1376260
  39.3 18.7 %copy-start.33 = (f32[7,128,128]{2,1,0:T(8,128)S(1)}, f32[7,128,128]{2,1,0:T(8,128)}, u32[]{:S(2)}) copy-start(f32[7,128,128]{2,1,0:T(8,128)} %constant_dynamic-update-slice_fusion) | copy-start | bytes 1376260
  39.3 18.7 %copy-start.42 = (f32[7,1,128]{2,1,0:T(1,128)S(1)}, f32[7,1,128]{2,1,0:T(1,128)}, u32[]{:S(2)}) copy-start(f32[7,1,128]{2,1,0:T(1,128)} %copy-done.41) | copy-start | bytes 10756
  39.4 18.7 %copy-start.43 = (f32[7]{0:T(128)S(1)}, f32[7]{0:T(128)}, u32[]{:S(2)}) copy-start(f32[7]{0:T(128)} %constant.10.clone) | copy-start | bytes 88
  40.3 17.7 %copy-start.40 = (f32[7,1,128]{2,1,0:T(1,128)S(1)}, f32[7,1,128]{2,1,0:T(1,128)}, u32[]{:S(2)}) copy-start(f32[7,1,128]{2,1,0:T(1,128)} %copy-done.39) | copy-start | bytes 10756
  40.3 27.9 %collective-permute-start.5 = (f32[2,7,130,1]{2,1,3,0:T(8,128)}, f32[2,7,130,1]{2,1,3,0:T(8,128)S(1)}, u32[]{:S(2)}, u32[]{:S(2)}) collective-permute-start(f32[2,7,130,1]{2,1,3,0:T(8,128)} %get-tuple-element.37), channel_id=1, source_target_pairs={{0,1},{1,2},{2,3},{3,4},{4,5},{5,6},{6,7},{8,9},{9,10},{10,11},{11... | collective-permute-start | bytes 21848 | tf_op jit(solution)/shard_map/ppermute | solution.py:24
  44.0 24.3 %collective-permute-start.7 = (f32[2,7,130,1]{2,1,3,0:T(8,128)}, f32[2,7,130,1]{2,1,3,0:T(8,128)}, u32[]{:S(2)}, u32[]{:S(2)}) collective-permute-start(f32[2,7,130,1]{2,1,3,0:T(8,128)} %get-tuple-element.38), channel_id=1, source_target_pairs={{1,0},{2,1},{3,2},{4,3},{5,4},{6,5},{7,6},{9,8},{10,9},{11,10},{12... | collective-permute-start | bytes 21848 | tf_op jit(solution)/shard_map/ppermute | solution.py:25
  73.6 88.9 %copy-start.1 = (f32[2,7,128,128]{2,1,3,0:T(8,128)}, f32[2,7,128,128]{2,1,3,0:T(8,128)S(1)}, u32[]{:S(2)}) copy-start(f32[2,7,128,128]{2,1,3,0:T(8,128)S(1)} %get-tuple-element.25) | copy-start | bytes 2752516
  76.5 3.8 %collective-permute-start.8 = (f32[2,7,1,128]{3,1,2,0:T(8,128)S(1)}, f32[2,7,1,128]{3,1,2,0:T(8,128)S(1)}, u32[]{:S(2)}, u32[]{:S(2)}) collective-permute-start(f32[2,7,1,128]{3,1,2,0:T(8,128)S(1)} %copy.140), channel_id=1, source_target_pairs={{0,8},{8,16},{16,24},{1,9},{9,17},{17,25},{2,10},{10,18},{18,26},{... | collective-permute-start | bytes 21512 | tf_op jit(solution)/shard_map/ppermute | solution.py:24
  79.0 3.1 %collective-permute-start.9 = (f32[2,7,1,128]{3,1,2,0:T(8,128)S(1)}, f32[2,7,1,128]{3,1,2,0:T(8,128)S(1)}, u32[]{:S(2)}, u32[]{:S(2)}) collective-permute-start(f32[2,7,1,128]{3,1,2,0:T(8,128)S(1)} %copy.142), channel_id=1, source_target_pairs={{8,0},{16,8},{24,16},{9,1},{17,9},{25,17},{10,2},{18,10},{26,18},{... | collective-permute-start | bytes 21512 | tf_op jit(solution)/shard_map/ppermute | solution.py:25
  83.4 11.2 %copy-start.23 = (f32[2,7,1,128]{2,1,3,0:T(8,128)S(1)}, f32[2,7,1,128]{2,1,3,0:T(8,128)}, u32[]{:S(2)}) copy-start(f32[2,7,1,128]{2,1,3,0:T(8,128)} %copy.143) | copy-start | bytes 21508
  84.4 6.1 %collective-permute-start.10 = (f32[2,7,130,1]{2,1,3,0:T(8,128)S(1)}, f32[2,7,130,1]{2,1,3,0:T(8,128)S(1)}, u32[]{:S(2)}, u32[]{:S(2)}) collective-permute-start(f32[2,7,130,1]{2,1,3,0:T(8,128)S(1)} %get-tuple-element.35), channel_id=1, source_target_pairs={{0,1},{1,2},{2,3},{3,4},{4,5},{5,6},{6,7},{8,9},{9,10},{10,11},{11... | collective-permute-start | bytes 21848 | tf_op jit(solution)/shard_map/ppermute | solution.py:24
  88.7 5.9 %collective-permute-start.11 = (f32[2,7,130,1]{2,1,3,0:T(8,128)S(1)}, f32[2,7,130,1]{2,1,3,0:T(8,128)S(1)}, u32[]{:S(2)}, u32[]{:S(2)}) collective-permute-start(f32[2,7,130,1]{2,1,3,0:T(8,128)S(1)} %get-tuple-element.36), channel_id=1, source_target_pairs={{1,0},{2,1},{3,2},{4,3},{5,4},{6,5},{7,6},{9,8},{10,9},{11,10},{12... | collective-permute-start | bytes 21848 | tf_op jit(solution)/shard_map/ppermute | solution.py:25
  143.3 4.3 %collective-permute-start.12 = (f32[2,7,1,128]{3,1,2,0:T(8,128)S(1)}, f32[2,7,1,128]{3,1,2,0:T(8,128)S(1)}, u32[]{:S(2)}, u32[]{:S(2)}) collective-permute-start(f32[2,7,1,128]{3,1,2,0:T(8,128)S(1)} %copy.147), channel_id=1, source_target_pairs={{0,8},{8,16},{16,24},{1,9},{9,17},{17,25},{2,10},{10,18},{18,26},{... | collective-permute-start | bytes 21512 | tf_op jit(solution)/shard_map/ppermute | solution.py:24
  146.1 5.6 %collective-permute-start.13 = (f32[2,7,1,128]{3,1,2,0:T(8,128)S(1)}, f32[2,7,1,128]{3,1,2,0:T(8,128)S(1)}, u32[]{:S(2)}, u32[]{:S(2)}) collective-permute-start(f32[2,7,1,128]{3,1,2,0:T(8,128)S(1)} %copy.149), channel_id=1, source_target_pairs={{8,0},{16,8},{24,16},{9,1},{17,9},{25,17},{10,2},{18,10},{26,18},{... | collective-permute-start | bytes 21512 | tf_op jit(solution)/shard_map/ppermute | solution.py:25
  153.1 9.4 %copy-start.28 = (f32[2,7,1,128]{2,1,3,0:T(8,128)S(1)}, f32[2,7,1,128]{2,1,3,0:T(8,128)}, u32[]{:S(2)}) copy-start(f32[2,7,1,128]{2,1,3,0:T(8,128)} %copy.150) | copy-start | bytes 21508
  154.1 4.3 %collective-permute-start.14 = (f32[2,7,130,1]{2,1,3,0:T(8,128)S(1)}, f32[2,7,130,1]{2,1,3,0:T(8,128)S(1)}, u32[]{:S(2)}, u32[]{:S(2)}) collective-permute-start(f32[2,7,130,1]{2,1,3,0:T(8,128)S(1)} %get-tuple-element.33), channel_id=1, source_target_pairs={{0,1},{1,2},{2,3},{3,4},{4,5},{5,6},{6,7},{8,9},{9,10},{10,11},{11... | collective-permute-start | bytes 21848 | tf_op jit(solution)/shard_map/ppermute | solution.py:24
  156.6 5.9 %collective-permute-start.15 = (f32[2,7,130,1]{2,1,3,0:T(8,128)S(1)}, f32[2,7,130,1]{2,1,3,0:T(8,128)S(1)}, u32[]{:S(2)}, u32[]{:S(2)}) collective-permute-start(f32[2,7,130,1]{2,1,3,0:T(8,128)S(1)} %get-tuple-element.34), channel_id=1, source_target_pairs={{1,0},{2,1},{3,2},{4,3},{5,4},{6,5},{7,6},{9,8},{10,9},{11,10},{12... | collective-permute-start | bytes 21848 | tf_op jit(solution)/shard_map/ppermute | solution.py:25
  215.9 7.9 %collective-permute-start.17 = (f32[2,7,1,128]{3,1,2,0:T(8,128)S(1)}, f32[2,7,1,128]{3,1,2,0:T(8,128)S(1)}, u32[]{:S(2)}, u32[]{:S(2)}) collective-permute-start(f32[2,7,1,128]{3,1,2,0:T(8,128)S(1)} %copy.155), channel_id=1, source_target_pairs={{8,0},{16,8},{24,16},{9,1},{17,9},{25,17},{10,2},{18,10},{26,18},{... | collective-permute-start | bytes 21512 | tf_op jit(solution)/shard_map/ppermute | solution.py:25
  217.2 5.2 %collective-permute-start.16 = (f32[2,7,1,128]{3,1,2,0:T(8,128)S(1)}, f32[2,7,1,128]{3,1,2,0:T(8,128)S(1)}, u32[]{:S(2)}, u32[]{:S(2)}) collective-permute-start(f32[2,7,1,128]{3,1,2,0:T(8,128)S(1)} %copy.153), channel_id=1, source_target_pairs={{0,8},{8,16},{16,24},{1,9},{9,17},{17,25},{2,10},{10,18},{18,26},{... | collective-permute-start | bytes 21512 | tf_op jit(solution)/shard_map/ppermute | solution.py:24
  225.1 10.8 %copy-start.18 = (f32[7,128,128]{1,0,2:T(8,128)S(1)}, f32[7,128,128]{1,0,2:T(8,128)}, u32[]{:S(2)}) copy-start(f32[7,128,128]{1,0,2:T(8,128)} %copy.134) | copy-start | bytes 1376260
  225.1 10.8 %copy-start.21 = (f32[7,128,128]{1,0,2:T(8,128)S(1)}, f32[7,128,128]{1,0,2:T(8,128)}, u32[]{:S(2)}) copy-start(f32[7,128,128]{1,0,2:T(8,128)} %copy.117) | copy-start | bytes 1376260
  226.1 5.8 %collective-permute-start.18 = (f32[2,7,130,1]{2,1,3,0:T(8,128)S(1)}, f32[2,7,130,1]{2,1,3,0:T(8,128)S(1)}, u32[]{:S(2)}, u32[]{:S(2)}) collective-permute-start(f32[2,7,130,1]{2,1,3,0:T(8,128)S(1)} %get-tuple-element.31), channel_id=1, source_target_pairs={{0,1},{1,2},{2,3},{3,4},{4,5},{5,6},{6,7},{8,9},{9,10},{10,11},{11... | collective-permute-start | bytes 21848 | tf_op jit(solution)/shard_map/ppermute | solution.py:24
  230.3 5.6 %collective-permute-start.19 = (f32[2,7,130,1]{2,1,3,0:T(8,128)S(1)}, f32[2,7,130,1]{2,1,3,0:T(8,128)S(1)}, u32[]{:S(2)}, u32[]{:S(2)}) collective-permute-start(f32[2,7,130,1]{2,1,3,0:T(8,128)S(1)} %get-tuple-element.32), channel_id=1, source_target_pairs={{1,0},{2,1},{3,2},{4,3},{5,4},{6,5},{7,6},{9,8},{10,9},{11,10},{12... | collective-permute-start | bytes 21848 | tf_op jit(solution)/shard_map/ppermute | solution.py:25
  (33 other events, 155.0 us)
where the time goes:
time: 285 us; the launch traced here: 284 us
  blocking collectives  123 us (43%)
  starting transfers between devices  48.3 us (17%)
  local copies, waits for them, and re-layouts  47.9 us (17%)
  other arithmetic  35.5 us (12%)
  waiting for transfers between devices  28.2 us (10%)
    psum x3, blocking collectives, both_sums(): lax.psum((core_sum(residual, scaled), core_sum(scaled, image)), ('gx', 'g...  123 us
    ppermute x10, starting transfers between devices, extended_2(): before = lax.ppermute(last, axis, up)  34.7 us
    ppermute x10, waiting for transfers between devices, extended_2(): after = lax.ppermute(leading, axis, down)  16.7 us
    ppermute x10, starting transfers between devices, extended_2(): after = lax.ppermute(leading, axis, down)  13.6 us
    ppermute x10, waiting for transfers between devices, extended_2(): before = lax.ppermute(last, axis, up)  11.5 us
    reduce_sum x4, other arithmetic, core_sum(): return jnp.sum(first * second, axis=(1, 2, 3))  10.6 us
    div x3, other arithmetic, per_device(): scaled = residual / diagonal  10.3 us
    slice x7, local copies, waits for them, and re-layouts, extended_2(): last = lax.slice_in_dim(x, length - width, length, axis=dim)  10.2 us
  transfers between devices with their start and end apart: 20, of which 7 were waited for; matrix products, arithmetic and copies ran while one was open for 13% of the time, Pallas kernels for 0%

commit v1 on v0

v1 whole, which is shorter than its diff:
```python
import functools
import math

import jax
import jax.numpy as jnp
from jax import lax
from jax.experimental import pallas as pl
from jax.experimental.pallas import tpu as pltpu
from jax.sharding import PartitionSpec as P

ITERS = 3
TIER_K = (1.0, 0.3, 0.12, 2.5)
CHANNEL_K = (1.0, 0.3, 0.25, 0.2)
CHANNEL_SINK = (0.0, 0.15, 0.45, 1.2)
TIER_HEAT = 0.05
CHANNEL_HEAT = 0.2
VERTICAL = 4.0

HALO = 8
STRIP = 4
SLOT = 2 * STRIP
MESH = pl.DeviceIdType.MESH

TIER_ROOT = tuple(math.sqrt(v) for v in TIER_K)
CHANNEL_ROOT = tuple(math.sqrt(v) for v in CHANNEL_K)
TIER_INV = tuple(1.0 / math.sqrt(v) for v in TIER_K)
CHANNEL_INV = tuple(1.0 / math.sqrt(v) for v in CHANNEL_K)


def lookup(codes, table):
    total = jnp.zeros(codes.shape, jnp.float32)
    for index, value in enumerate(table):
        total = jnp.where(codes == index, jnp.float32(value), total)
    return total


def coefficients(nu):
    def inner(a, b):
        total = None
        for i, x in enumerate(a):
            for j, y in enumerate(b):
                term = x * y * nu[i + j]
                total = term if total is None else total + term
        return total

    zero = nu[0] * 0.0
    rho = [zero + 1.0]
    pi = [zero + 1.0]
    norm = nu[0]
    result = [zero] * ITERS
    for iteration in range(ITERS):
        image = [a - b for a, b in zip(pi + [zero], [zero] + pi)]
        step = norm / inner(pi, image)
        for i, a in enumerate(pi):
            result[i] = result[i] + step * a
        if iteration + 1 < ITERS:
            rho = [a - step * b for a, b in zip(rho + [zero], image)]
            following = inner(rho, rho)
            growth = following / norm
            pi = [a + growth * b for a, b in zip(rho, pi + [zero])]
            norm = following
    return result


def kernel(nx, ny, prev, diss, mat, cool, out, vp, vq, vm, vc, own_l, own_r, far_l, far_r,
           edges, root, weight, capac, up, u0, u1, u2, result, row, rows,
           load_sem, send_sem, recv_sem, row_send, row_recv, store_sem):
    scen, layers, length, width = prev.shape
    tiers = mat.shape[0]
    n = nx * ny
    ext = length + 2 * HALO
    x, y = lax.axis_index("gx"), lax.axis_index("gy")
    me = x * ny + y
    barrier = pltpu.get_barrier_semaphore()

    def other(i):
        k = lax.rem(me + i, n)
        return k // ny, lax.rem(k, ny)

    def greet(i, carry):
        pl.semaphore_signal(barrier, inc=1, device_id=other(i), device_id_type=MESH)
        return carry

    inside = pl.ds(HALO, length)
    loads = [
        pltpu.make_async_copy(prev, vp.at[:, :, inside], load_sem.at[0]),
        pltpu.make_async_copy(diss, vq.at[:, :, inside], load_sem.at[1]),
        pltpu.make_async_copy(mat, vm.at[:, inside], load_sem.at[2]),
        pltpu.make_async_copy(cool, vc.at[:, inside], load_sem.at[3]),
    ]
    for copy in loads:
        copy.start()
    lax.fori_loop(1, n, greet, 0)

    has = {(-1, 0): x > 0, (1, 0): x < nx - 1, (0, -1): y > 0, (0, 1): y < ny - 1}
    for dx in (-1, 1):
        for dy in (-1, 1):
            has[dx, dy] = jnp.logical_and(has[dx, 0], has[0, dy])
    top, bottom = pl.ds(0, HALO), pl.ds(HALO + length, HALO)
    first, last = pl.ds(HALO, HALO), pl.ds(length, HALO)

    def fill(ref):
        ref[...] = jnp.full(ref.shape, -1, ref.dtype)

    for dx, where in ((-1, top), (1, bottom)):
        @pl.when(jnp.logical_not(has[dx, 0]))
        def _(where=where):
            for ref in (vp, vq):
                fill(ref.at[:, :, where])
            for ref in (vm, vc):
                fill(ref.at[:, where])
            fill(own_l.at[where])
            fill(own_r.at[where])
    for dy, ref in ((-1, far_l), (1, far_r)):
        @pl.when(jnp.logical_not(has[0, dy]))
        def _(ref=ref):
            fill(ref.at[inside])
        for dx, where in ((-1, top), (1, bottom)):
            @pl.when(jnp.logical_not(has[dx, dy]))
            def _(ref=ref, where=where):
                fill(ref.at[where])

    for copy in loads:
        copy.wait()

    places = []
    for s in range(scen):
        for layer in range(layers):
            places.append((SLOT * (s * layers + layer), vp, (s, layer)))
    for layer in range(layers):
        ref = vm if layer % 2 == 0 else vc
        places.append((SLOT * layer + STRIP, ref, (layer // 2,)))
    for t in range(tiers):
        places.append((SLOT * (layers + 1 + 2 * t) + STRIP, vq, (0, t)))
        places.append((SLOT * (layers + 2 * t) + STRIP, vq, (1, t)))
    chunk = 4 * HALO

    def pack(step, carry):
        start = pl.multiple_of(HALO + step * chunk, HALO)
        lane = lax.broadcasted_iota(jnp.int32, (chunk, width), 1)
        left = jnp.zeros((chunk, width), jnp.float32)
        right = jnp.zeros((chunk, width), jnp.float32)
        for base, ref, index in places:
            plane = ref[index + (pl.ds(start, chunk),)].astype(jnp.float32)
            turned = pltpu.roll(plane, base, 1) if base else plane
            left = jnp.where((lane >= base) & (lane < base + STRIP), turned, left)
            low = (base - STRIP) % width
            right = jnp.where((lane >= low) & (lane < low + STRIP), turned, right)
        own_l[pl.ds(start, chunk)] = left
        own_r[pl.ds(start, chunk)] = pltpu.roll(right, STRIP, 1)
        return carry

    lax.fori_loop(0, length // chunk, pack, 0)

    pl.semaphore_wait(barrier, n - 1)

    sends = []
    for dx, source, target in ((-1, first, bottom), (1, last, top)):
        for ref in (vp, vq):
            sends.append((dx, 0, ref.at[:, :, source], ref.at[:, :, target]))
        for ref in (vm, vc):
            sends.append((dx, 0, ref.at[:, source], ref.at[:, target]))
        for ref in (own_l, own_r):
            sends.append((dx, 0, ref.at[source], ref.at[target]))
        sends.append((dx, -1, own_l.at[source], far_r.at[target]))
        sends.append((dx, 1, own_r.at[source], far_l.at[target]))
    sends.append((0, -1, own_l.at[inside], far_r.at[inside]))
    sends.append((0, 1, own_r.at[inside], far_l.at[inside]))
    copies = []
    for i, (dx, dy, source, target) in enumerate(sends):
        copy = pltpu.make_async_remote_copy(
            src_ref=source, dst_ref=target, send_sem=send_sem.at[i], recv_sem=recv_sem.at[i],
            device_id=(x + dx, y + dy), device_id_type=MESH)
        copies.append((dx, dy, copy))
    order = sorted(copies, key=lambda c: 0 if c[0] == 0 else 1 if c[1] == 0 else 2)
    for dx, dy, copy in order:
        @pl.when(has[dx, dy])
        def _(copy=copy):
            copy.start()
    for dx, dy, copy in copies:
        @pl.when(has[-dx, -dy])
        def _(copy=copy):
            copy.wait_recv()

    shape = (ext, width)
    lane = lax.broadcasted_iota(jnp.int32, shape, 1)
    place = lane // SLOT
    low = lane % SLOT < STRIP
    layer_of = place % layers
    tier = layer_of % 2 == 0
    used = place < scen * layers

    def strip_stencil(u):
        lateral = pltpu.roll(u, 1, 1) + pltpu.roll(u, width - 1, 1)
        lateral = lateral + pltpu.roll(u, 1, 0) + pltpu.roll(u, ext - 1, 0)
        above = jnp.where(layer_of > 0, pltpu.roll(u, SLOT, 1), 0.0)
        below = jnp.where(layer_of < layers - 1, pltpu.roll(u, width - SLOT, 1), 0.0)
        return lateral + VERTICAL * (above + below)

    def strip(field, rest):
        codes = jnp.where(place < layers, rest, pltpu.roll(rest, SLOT * layers, 1))
        codes = jnp.where(used, codes, -1.0)
        power = jnp.where(place < layers, pltpu.roll(rest, width - SLOT * (layers + 1), 1), rest)
        power = jnp.where(tier & used, power, 0.0)
        s = jnp.where(tier, lookup(codes, TIER_ROOT), lookup(codes, CHANNEL_ROOT))
        heat = jnp.where(tier, TIER_HEAT, CHANNEL_HEAT)
        total = heat + jnp.where(tier, 0.0, lookup(codes, CHANNEL_SINK))
        total = total + s * strip_stencil(s)
        inverse = 1.0 / total
        scaled = s * field
        residual = (heat - total) * field + power + s * strip_stencil(scaled)
        w = s * s * inverse
        a = s * residual * inverse
        b = w * strip_stencil(a)
        c = w * strip_stencil(b)
        return s, scaled, a, b, c

    here, there = own_l[...], far_l[...]
    lefts = strip(jnp.where(low, there, pltpu.roll(here, STRIP, 1)),
                  jnp.where(low, pltpu.roll(there, width - STRIP, 1), here))
    for i, value in enumerate(lefts):
        edges[i] = value
    here, there = own_r[...], far_r[...]
    rights = strip(jnp.where(low, here, pltpu.roll(there, STRIP, 1)),
                   jnp.where(low, pltpu.roll(here, width - STRIP, 1), there))
    for i, value in enumerate(rights):
        edges[i] = jnp.where(lane % SLOT == STRIP - 1, edges[i], pltpu.roll(value, width - 2, 1))

    body = pl.ds(HALO, ext)
    blank = jnp.zeros((ext + 2 * HALO, width), jnp.float32)
    for pad in (0, layers + 1):
        root[pad] = blank
        for s in range(scen):
            for ref in (up, u0, u1, u2):
                ref[s, pad] = blank
    for layer in range(layers):
        if layer % 2 == 0:
            s = lookup(vm[layer // 2], TIER_ROOT)
            total = jnp.full(shape, TIER_HEAT, jnp.float32)
        else:
            codes = vc[layer // 2]
            s = lookup(codes, CHANNEL_ROOT)
            total = CHANNEL_HEAT + lookup(codes, CHANNEL_SINK)
        root[layer + 1, body] = s
        capac[layer] = total
        for k in range(scen):
            up[k, layer + 1, body] = s * vp[k, layer]

    def stencil(ref, at, layer, edge, slot):
        centre = ref[at + (layer + 1, body)]
        border = pltpu.roll(edges[edge], lax.rem(2 * width - STRIP + 1 - SLOT * slot, width), 1)
        west = jnp.where(lane == 0, border, pltpu.roll(centre, 1, 1))
        east = jnp.where(lane == width - 1, border, pltpu.roll(centre, width - 1, 1))
        lateral = west + east + ref[at + (layer + 1, pl.ds(HALO - 1, ext))]
        lateral = lateral + ref[at + (layer + 1, pl.ds(HALO + 1, ext))]
        vertical = ref[at + (layer, body)] + ref[at + (layer + 2, body)]
        return centre, lateral + VERTICAL * vertical

    def gather(total, value):
        tiles = value[HALO:HALO + length].reshape(length // HALO, HALO, width)
        return total + jnp.sum(tiles, axis=0)

    none = jnp.zeros((HALO, width), jnp.float32)

    def begin(layer, carry):
        is_tier = lax.rem(layer, 2) == 0
        heat = jnp.where(is_tier, jnp.float32(TIER_HEAT), jnp.float32(CHANNEL_HEAT))
        on = jnp.where(is_tier, jnp.float32(1.0), jnp.float32(0.0))
        s, around = stencil(root, (), layer, 0, layer)
        total = capac[layer] + s * around
        inverse = 1.0 / total
        weight[layer] = s * s * inverse
        sums = []
        for k in range(scen):
            _, around = stencil(up, (k,), layer, 1, k * layers + layer)
            residual = (heat - total) * vp[k, layer] + on * vq[k, layer // 2] + s * around
            scaled = residual * inverse
            u0[k, layer + 1, body] = s * scaled
            sums.append(gather(carry[k], residual * scaled))
        return tuple(sums)

    def advance(source, target, edge):
        def one(layer, carry):
            sums = []
            for k in range(scen):
                centre, around = stencil(source, (k,), layer, edge, k * layers + layer)
                sums.append(gather(carry[len(sums)], centre * around))
                if target is not None:
                    moved = weight[layer] * around
                    target[k, layer + 1, body] = moved
                    sums.append(gather(carry[len(sums)], moved * around))
            return tuple(sums)

        count = scen * (1 if target is None else 2)
        return lax.fori_loop(0, layers, one, (none,) * count)

    first_sums = lax.fori_loop(0, layers, begin, (none,) * scen)
    second = advance(u0, u1, 2)
    third = advance(u1, u2, 3)
    fourth = advance(u2, None, 4)
    moments = []
    for k in range(scen):
        moments += [first_sums[k], *second[2 * k:2 * k + 2], *third[2 * k:2 * k + 2], fourth[k]]
    count = len(moments)
    flat = jnp.zeros((1, width), jnp.float32)
    line = lax.broadcasted_iota(jnp.int32, (1, width), 1)
    for i, value in enumerate(moments):
        total = jnp.sum(jnp.sum(value, axis=0, keepdims=True), axis=1, keepdims=True)
        flat = jnp.where(line == i, total, flat)
    row[...] = flat
    rows[n - 1] = flat

    def to(i):
        return pltpu.make_async_remote_copy(
            src_ref=row, dst_ref=rows.at[i - 1], send_sem=row_send, recv_sem=row_recv,
            device_id=other(i), device_id_type=MESH)

    def spread(i, carry):
        to(i).start()
        return carry

    lax.fori_loop(1, n, spread, 0)
    for dx, dy, copy in copies:
        @pl.when(has[dx, dy])
        def _(copy=copy):
            copy.wait_send()
    arrived = rows.at[pl.ds(0, n - 1)]
    pltpu.make_async_copy(arrived, arrived, row_recv).wait()
    summed = jnp.sum(rows[...], axis=0)
    total = [jnp.sum(jnp.where(line == i, summed, 0.0), axis=1, keepdims=True)
             for i in range(count)]
    each = count // scen
    for k in range(scen):
        c0, c1, c2 = coefficients(total[k * each:(k + 1) * each])
        own = pl.ds(2 * HALO, length)
        for layer in range(layers):
            if layer % 2 == 0:
                back = lookup(vm[layer // 2, inside], TIER_INV)
            else:
                back = lookup(vc[layer // 2, inside], CHANNEL_INV)
            change = c0 * u0[k, layer + 1, own] + c1 * u1[k, layer + 1, own]
            change = change + c2 * u2[k, layer + 1, own]
            result[k, layer] = vp[k, layer, inside] + back * change
        pltpu.make_async_copy(result.at[k], out.at[k], store_sem.at[k]).start()
    for k in range(scen):
        pltpu.make_async_copy(result.at[k], out.at[k], store_sem.at[k]).wait()
    pltpu.make_async_copy(arrived, arrived, row_send).wait()


def per_device(nx, ny, previous, dissipated, material, coolant):
    scen, layers, length, width = previous.shape
    tiers = material.shape[0]
    ext = length + 2 * HALO
    f32 = jnp.float32
    field = pltpu.VMEM((scen, layers + 2, ext + 2 * HALO, width), f32)
    strip = pltpu.VMEM((ext, width), f32)
    return pl.pallas_call(
        functools.partial(kernel, nx, ny),
        out_shape=jax.ShapeDtypeStruct(previous.shape, f32),
        in_specs=[pl.BlockSpec(memory_space=pl.ANY)] * 4,
        out_specs=pl.BlockSpec(memory_space=pl.ANY),
        scratch_shapes=[
            pltpu.VMEM((scen, layers, ext, width), f32),
            pltpu.VMEM((scen, tiers, ext, width), f32),
            pltpu.VMEM((tiers, ext, width), jnp.int32),
            pltpu.VMEM((layers - tiers, ext, width), jnp.int32),
            strip, strip, strip, strip,
            pltpu.VMEM((5, ext, width), f32),
            pltpu.VMEM((layers + 2, ext + 2 * HALO, width), f32),
            pltpu.VMEM((layers, ext, width), f32),
            pltpu.VMEM((layers, ext, width), f32),
            field, field, field, field,
            pltpu.VMEM(previous.shape, f32),
            pltpu.VMEM((1, width), f32),
            pltpu.VMEM((nx * ny, 1, width), f32),
            pltpu.SemaphoreType.DMA((4,)),
            pltpu.SemaphoreType.DMA((18,)),
            pltpu.SemaphoreType.DMA((18,)),
            pltpu.SemaphoreType.DMA,
            pltpu.SemaphoreType.DMA,
            pltpu.SemaphoreType.DMA((scen,)),
        ],
        compiler_params=pltpu.CompilerParams(
            collective_id=0, has_side_effects=True, vmem_limit_bytes=40 * 1024 * 1024),
    )(previous, dissipated, material, coolant)


def solution(mesh):
    return jax.shard_map(
        functools.partial(per_device, mesh.shape["gx"], mesh.shape["gy"]),
        mesh=mesh,
        in_specs=(
            P(None, None, "gx", "gy"),
            P(None, None, "gx", "gy"),
            P(None, "gx", "gy"),
            P(None, "gx", "gy"),
        ),
        out_specs=P(None, None, "gx", "gy"),
        check_vma=False,
    )
```

time: 285 us -> 30.8 us (0.11)
  blocking collectives: 123 us -> 0 us
  starting transfers between devices: 48.3 us -> 0 us
  local copies, waits for them, and re-layouts: 47.9 us -> 5.02 us
  other arithmetic: 35.5 us -> 0 us
  waiting for transfers between devices: 28.2 us -> 0 us
  Pallas kernels: 0 us -> 25.5 us
    psum x3 -> x0, blocking collectives: 123 us -> none  [both_sums(): lax.psum((core_sum(residual, scaled), core_sum(scaled, image)), ('gx', 'g...]
    ppermute x20 -> x0, starting transfers between devices: 48.3 us -> none  [the longest x10 34.7 us: extended_2(): before = lax.ppermute(last, axis, up)]
    ppermute x20 -> x0, waiting for transfers between devices: 28.2 us -> none  [the longest x10 16.7 us: extended_2(): after = lax.ppermute(leading, axis, down)]
    pallas_call x0 -> x1, Pallas kernels: none -> 25.5 us  [per_device(): pl.pallas_call(functools.partial(kernel, nx, ny), out_shape=jax.ShapeDtyp...]
    slice x17 -> x0, local copies, waits for them, and re-layouts: 15.8 us -> none  [the longest x7 10.2 us: extended_2(): last = lax.slice_in_dim(x, length - width, length, axis=dim)]
    reduce_sum x4 -> x0, other arithmetic: 10.6 us -> none  [core_sum(): return jnp.sum(first * second, axis=(1, 2, 3))]
    div x6 -> x0, other arithmetic: 10.3 us -> none  [the longest x3 10.3 us: per_device(): scaled = residual / diagonal]
    ppermute x8 -> x0, local copies, waits for them, and re-layouts: 9.71 us -> none  [the longest x4 5.22 us: extended_2(): before = lax.ppermute(last, axis, up)]
  transfers between devices with their start and end apart: 20 -> 0, of which waited for: 7 -> 0; matrix products, arithmetic and copies ran while one was open for 13% -> 0% of each run, Pallas kernels for 0% -> 0%
where the time goes in v1:
time: 30.8 us; the launch traced here: 30.6 us
  Pallas kernels  25.5 us (83%)
  local copies, waits for them, and re-layouts  5.02 us (16%)
    pallas_call x1, Pallas kernels, per_device(): pl.pallas_call(functools.partial(kernel, nx, ny), out_shape=jax.ShapeDtyp...  25.5 us
    unnamed x9, local copies, waits for them, and re-layouts  5.02 us

profile of v1, /device:TPU:0, one launch (start us, length us, event | category | flops | bytes accessed | tf_op | source)
XLA Modules:
  0.0 30.6 jit_solution(1562539978342700977)
XLA Ops:
  0.0 0.0 copy-start
  0.0 1.2 %copy-done = f32[2,7,128,128]{3,2,1,0:T(8,128)S(1)} copy-done((f32[2,7,128,128]{3,2,1,0:T(8,128)S(1)}, f32[2,7,128,128]{3,2,1,0:T(8,128)}, u32[]{:S(2)}) %copy-start) | copy-done | bytes 917528
  1.2 0.0 copy-start.1
  1.2 1.0 %copy-done.1 = f32[2,4,128,128]{3,2,1,0:T(8,128)S(1)} copy-done((f32[2,4,128,128]{3,2,1,0:T(8,128)S(1)}, f32[2,4,128,128]{3,2,1,0:T(8,128)}, u32[]{:S(2)}) %copy-start.1) | copy-done | bytes 524312
  2.2 0.0 copy-start.2
  2.2 0.9 %copy-done.2 = s32[4,128,128]{2,1,0:T(8,128)S(1)} copy-done((s32[4,128,128]{2,1,0:T(8,128)S(1)}, s32[4,128,128]{2,1,0:T(8,128)}, u32[]{:S(2)}) %copy-start.2) | copy-done | bytes 262168
  3.2 0.0 copy-start.3
  3.2 0.9 %copy-done.3 = s32[3,128,128]{2,1,0:T(8,128)S(1)} copy-done((s32[3,128,128]{2,1,0:T(8,128)S(1)}, s32[3,128,128]{2,1,0:T(8,128)}, u32[]{:S(2)}) %copy-start.3) | copy-done | bytes 196632
  4.1 25.5 %shard_map.46 = f32[2,7,128,128]{3,2,1,0:T(8,128)S(1)} custom-call(f32[2,7,128,128]{3,2,1,0:T(8,128)S(1)} %copy-done, f32[2,4,128,128]{3,2,1,0:T(8,128)S(1)} %copy-done.1, s32[4,128,128]{2,1,0:T(8,128)S(1)} %copy-done.2, s32[3,128,128]{2,1,0:T(8,128)S(1)} %copy-done.3), custom_call_target="tpu_custom_call" | custom-call | tf_op jit(solution)/shard_map/pallas_call | solution.py:357
  29.6 0.9 %copy.6 = f32[2,7,128,128]{3,2,1,0:T(8,128)} copy(f32[2,7,128,128]{3,2,1,0:T(8,128)S(1)} %shard_map.46) | data formatting | bytes 1835008
Async XLA Ops:
  0.0 1.2 %copy-start = (f32[2,7,128,128]{3,2,1,0:T(8,128)S(1)}, f32[2,7,128,128]{3,2,1,0:T(8,128)}, u32[]{:S(2)}) copy-start(f32[2,7,128,128]{3,2,1,0:T(8,128)} %prev.1) | copy-start | bytes 2752516
  1.2 1.0 %copy-start.1 = (f32[2,4,128,128]{3,2,1,0:T(8,128)S(1)}, f32[2,4,128,128]{3,2,1,0:T(8,128)}, u32[]{:S(2)}) copy-start(f32[2,4,128,128]{3,2,1,0:T(8,128)} %diss.1) | copy-start | bytes 1572868
  2.2 0.9 %copy-start.2 = (s32[4,128,128]{2,1,0:T(8,128)S(1)}, s32[4,128,128]{2,1,0:T(8,128)}, u32[]{:S(2)}) copy-start(s32[4,128,128]{2,1,0:T(8,128)} %mat.1) | copy-start | bytes 786436
  3.2 0.9 %copy-start.3 = (s32[3,128,128]{2,1,0:T(8,128)S(1)}, s32[3,128,128]{2,1,0:T(8,128)}, u32[]{:S(2)}) copy-start(s32[3,128,128]{2,1,0:T(8,128)} %cool.1) | copy-start | bytes 589828

commit v2 on v1

--- a/solution.py
+++ b/solution.py
@@ -64,7 +64,7 @@
 
 def kernel(nx, ny, prev, diss, mat, cool, out, vp, vq, vm, vc, own_l, own_r, far_l, far_r,
            edges, root, weight, capac, up, u0, u1, u2, result, row, rows,
-           load_sem, send_sem, recv_sem, row_send, row_recv, store_sem):
+           picks, split, load_sem, send_sem, recv_sem, row_send, row_recv, store_sem):
     scen, layers, length, width = prev.shape
     tiers = mat.shape[0]
     n = nx * ny
@@ -151,6 +151,17 @@
         return carry
 
     lax.fori_loop(0, length // chunk, pack, 0)
+
+    def pick(slot, carry):
+        near = (2 * width, width)
+        source = lax.broadcasted_iota(jnp.int32, near, 0) % width - SLOT * slot
+        target = lax.broadcasted_iota(jnp.int32, near, 1)
+        west = (source == STRIP - 1) & (target == 0)
+        east = (source == STRIP - 2) & (target == width - 1)
+        picks[slot] = jnp.where(west | east, 1.0, 0.0).astype(jnp.bfloat16)
+        return carry
+
+    lax.fori_loop(0, scen * layers, pick, 0)
 
     pl.semaphore_wait(barrier, n - 1)
 
@@ -177,10 +188,67 @@
         @pl.when(has[dx, dy])
         def _(copy=copy):
             copy.start()
+    blank = jnp.zeros((ext + 2 * HALO, width), jnp.float32)
+    for pad in (0, layers + 1):
+        root[pad] = blank
+        for s in range(scen):
+            for ref in (up, u0, u1, u2):
+                ref[s, pad] = blank
+
+    def prepare(begin, count):
+        at, to = pl.ds(begin, count), pl.ds(begin + HALO, count)
+        for layer in range(layers):
+            if layer % 2 == 0:
+                s = lookup(vm[layer // 2, at], TIER_ROOT)
+                total = jnp.full((count, width), TIER_HEAT, jnp.float32)
+            else:
+                codes = vc[layer // 2, at]
+                s = lookup(codes, CHANNEL_ROOT)
+                total = CHANNEL_HEAT + lookup(codes, CHANNEL_SINK)
+            root[layer + 1, to] = s
+            capac[layer, at] = total
+            for k in range(scen):
+                up[k, layer + 1, to] = s * vp[k, layer, at]
+
+    prepare(HALO, length)
+    body = pl.ds(HALO, ext)
+
+    def stencil(ref, at, layer, edge, slot, start=0, count=ext):
+        lane = lax.broadcasted_iota(jnp.int32, (count, width), 1)
+        rows_at = pl.ds(HALO + start, count)
+        centre = ref[at + (layer + 1, rows_at)]
+        west = jnp.where(lane == 0, 0.0, pltpu.roll(centre, 1, 1))
+        east = jnp.where(lane == width - 1, 0.0, pltpu.roll(centre, width - 1, 1))
+        lateral = west + east + ref[at + (layer + 1, pl.ds(HALO + start - 1, count))]
+        lateral = lateral + ref[at + (layer + 1, pl.ds(HALO + start + 1, count))]
+        vertical = ref[at + (layer, rows_at)] + ref[at + (layer + 2, rows_at)]
+        around = lateral + VERTICAL * vertical
+        if edge is not None:
+            around = around + border(edge, slot, start, count)
+        return centre, around
+
+    def border(edge, slot, start, count):
+        return jnp.dot(split[edge, pl.ds(start, count)], picks[slot],
+                       preferred_element_type=jnp.float32)
+
+    inner, rest = 2 * HALO, length - 2 * HALO
+
+    def early(layer, carry):
+        at = pl.ds(inner, rest)
+        weight[layer, at] = stencil(root, (), layer, None, 0, inner, rest)[1]
+        for k in range(scen):
+            u1[k, layer + 1, at] = stencil(up, (k,), layer, None, 0, inner, rest)[1]
+        return carry
+
+    lax.fori_loop(0, layers, early, 0)
+
     for dx, dy, copy in copies:
         @pl.when(has[-dx, -dy])
         def _(copy=copy):
             copy.wait_recv()
+
+    prepare(0, HALO)
+    prepare(HALO + length, HALO)
 
     shape = (ext, width)
     lane = lax.broadcasted_iota(jnp.int32, shape, 1)
@@ -224,37 +292,12 @@
     rights = strip(jnp.where(low, here, pltpu.roll(there, STRIP, 1)),
                    jnp.where(low, pltpu.roll(here, width - STRIP, 1), there))
     for i, value in enumerate(rights):
-        edges[i] = jnp.where(lane % SLOT == STRIP - 1, edges[i], pltpu.roll(value, width - 2, 1))
+        both = jnp.where(lane % SLOT == STRIP - 1, edges[i], pltpu.roll(value, width - 2, 1))
+        high = both.astype(jnp.bfloat16)
+        split[i, :, :width] = high
+        split[i, :, width:] = (both - high.astype(jnp.float32)).astype(jnp.bfloat16)
 
     body = pl.ds(HALO, ext)
-    blank = jnp.zeros((ext + 2 * HALO, width), jnp.float32)
-    for pad in (0, layers + 1):
-        root[pad] = blank
-        for s in range(scen):
-            for ref in (up, u0, u1, u2):
-                ref[s, pad] = blank
-    for layer in range(layers):
-        if layer % 2 == 0:
-            s = lookup(vm[layer // 2], TIER_ROOT)
-            total = jnp.full(shape, TIER_HEAT, jnp.float32)
-        else:
-            codes = vc[layer // 2]
-            s = lookup(codes, CHANNEL_ROOT)
-            total = CHANNEL_HEAT + lookup(codes, CHANNEL_SINK)
-        root[layer + 1, body] = s
-        capac[layer] = total
-        for k in range(scen):
-            up[k, layer + 1, body] = s * vp[k, layer]
-
-    def stencil(ref, at, layer, edge, slot):
-        centre = ref[at + (layer + 1, body)]
-        border = pltpu.roll(edges[edge], lax.rem(2 * width - STRIP + 1 - SLOT * slot, width), 1)
-        west = jnp.where(lane == 0, border, pltpu.roll(centre, 1, 1))
-        east = jnp.where(lane == width - 1, border, pltpu.roll(centre, width - 1, 1))
-        lateral = west + east + ref[at + (layer + 1, pl.ds(HALO - 1, ext))]
-        lateral = lateral + ref[at + (layer + 1, pl.ds(HALO + 1, ext))]
-        vertical = ref[at + (layer, body)] + ref[at + (layer + 2, body)]
-        return centre, lateral + VERTICAL * vertical
 
     def gather(total, value):
         tiles = value[HALO:HALO + length].reshape(length // HALO, HALO, width)
@@ -266,17 +309,30 @@
         is_tier = lax.rem(layer, 2) == 0
         heat = jnp.where(is_tier, jnp.float32(TIER_HEAT), jnp.float32(CHANNEL_HEAT))
         on = jnp.where(is_tier, jnp.float32(1.0), jnp.float32(0.0))
-        s, around = stencil(root, (), layer, 0, layer)
-        total = capac[layer] + s * around
-        inverse = 1.0 / total
-        weight[layer] = s * s * inverse
-        sums = []
-        for k in range(scen):
-            _, around = stencil(up, (k,), layer, 1, k * layers + layer)
-            residual = (heat - total) * vp[k, layer] + on * vq[k, layer // 2] + s * around
-            scaled = residual * inverse
-            u0[k, layer + 1, body] = s * scaled
-            sums.append(gather(carry[k], residual * scaled))
+        sums = list(carry)
+        for start, count in ((0, inner), (inner, rest), (inner + rest, inner)):
+            at = pl.ds(start, count)
+            if start == inner:
+                s = root[layer + 1, pl.ds(HALO + start, count)]
+                around = weight[layer, at] + border(0, layer, start, count)
+            else:
+                s, around = stencil(root, (), layer, 0, layer, start, count)
+            total = capac[layer, at] + s * around
+            inverse = 1.0 / total
+            weight[layer, at] = s * s * inverse
+            for k in range(scen):
+                slot = k * layers + layer
+                if start == inner:
+                    around = u1[k, layer + 1, at] + border(1, slot, start, count)
+                else:
+                    _, around = stencil(up, (k,), layer, 1, slot, start, count)
+                residual = (heat - total) * vp[k, layer, at] + on * vq[k, layer // 2, at]
+                residual = residual + s * around
+                scaled = residual * inverse
+                u0[k, layer + 1, pl.ds(HALO + start, count)] = s * scaled
+                own = residual * scaled
+                own = own[HALO:] if start == 0 else own[:HALO] if start > inner else own
+                sums[k] = sums[k] + jnp.sum(own.reshape(-1, HALO, width), axis=0)
         return tuple(sums)
 
     def advance(source, target, edge):
@@ -292,9 +348,9 @@
             return tuple(sums)
 
         count = scen * (1 if target is None else 2)
-        return lax.fori_loop(0, layers, one, (none,) * count)
-
-    first_sums = lax.fori_loop(0, layers, begin, (none,) * scen)
+        return lax.fori_loop(0, layers, one, (none,) * count, unroll=True)
+
+    first_sums = lax.fori_loop(0, layers, begin, (none,) * scen, unroll=True)
     second = advance(u0, u1, 2)
     third = advance(u1, u2, 3)
     fourth = advance(u2, None, 4)
@@ -324,6 +380,15 @@
         @pl.when(has[dx, dy])
         def _(copy=copy):
             copy.wait_send()
+    own = pl.ds(2 * HALO, length)
+    for layer in range(layers):
+        if layer % 2 == 0:
+            back = lookup(vm[layer // 2, inside], TIER_INV)
+        else:
+            back = lookup(vc[layer // 2, inside], CHANNEL_INV)
+        for k in range(scen):
+            for ref in (u0, u1, u2):
+                ref[k, layer + 1, own] = back * ref[k, layer + 1, own]
     arrived = rows.at[pl.ds(0, n - 1)]
     pltpu.make_async_copy(arrived, arrived, row_recv).wait()
     summed = jnp.sum(rows[...], axis=0)
@@ -332,18 +397,12 @@
     each = count // scen
     for k in range(scen):
         c0, c1, c2 = coefficients(total[k * each:(k + 1) * each])
-        own = pl.ds(2 * HALO, length)
         for layer in range(layers):
-            if layer % 2 == 0:
-                back = lookup(vm[layer // 2, inside], TIER_INV)
-            else:
-                back = lookup(vc[layer // 2, inside], CHANNEL_INV)
             change = c0 * u0[k, layer + 1, own] + c1 * u1[k, layer + 1, own]
             change = change + c2 * u2[k, layer + 1, own]
-            result[k, layer] = vp[k, layer, inside] + back * change
-        pltpu.make_async_copy(result.at[k], out.at[k], store_sem.at[k]).start()
-    for k in range(scen):
-        pltpu.make_async_copy(result.at[k], out.at[k], store_sem.at[k]).wait()
+            result[k, layer] = vp[k, layer, inside] + change
+            pltpu.make_async_copy(result.at[k, layer], out.at[k, layer], store_sem).start()
+    pltpu.make_async_copy(result, out, store_sem).wait()
     pltpu.make_async_copy(arrived, arrived, row_send).wait()
 
 
@@ -373,15 +432,17 @@
             pltpu.VMEM(previous.shape, f32),
             pltpu.VMEM((1, width), f32),
             pltpu.VMEM((nx * ny, 1, width), f32),
+            pltpu.VMEM((scen * layers, 2 * width, width), jnp.bfloat16),
+            pltpu.VMEM((5, ext, 2 * width), jnp.bfloat16),
             pltpu.SemaphoreType.DMA((4,)),
             pltpu.SemaphoreType.DMA((18,)),
             pltpu.SemaphoreType.DMA((18,)),
             pltpu.SemaphoreType.DMA,
             pltpu.SemaphoreType.DMA,
-            pltpu.SemaphoreType.DMA((scen,)),
+            pltpu.SemaphoreType.DMA,
         ],
         compiler_params=pltpu.CompilerParams(
-            collective_id=0, has_side_effects=True, vmem_limit_bytes=40 * 1024 * 1024),
+            collective_id=0, has_side_effects=True, vmem_limit_bytes=56 * 1024 * 1024),
     )(previous, dissipated, material, coolant)
 
 

time: 30.8 us -> 24.2 us (0.79)
  Pallas kernels: 25.5 us -> 21.8 us
  local copies, waits for them, and re-layouts: 5.02 us -> 2.18 us
    pallas_call x1, Pallas kernels: 25.5 us -> 21.8 us  [per_device(): pl.pallas_call(functools.partial(kernel, nx, ny), out_shape=jax.ShapeDtyp...]
    unnamed x9 -> x1, local copies, waits for them, and re-layouts: 5.02 us -> 2.18 us
where the time goes in v2:
time: 24.2 us; the launch traced here: 24 us
  Pallas kernels  21.8 us (90%)
  local copies, waits for them, and re-layouts  2.18 us (9%)
    pallas_call x1, Pallas kernels, per_device(): pl.pallas_call(functools.partial(kernel, nx, ny), out_shape=jax.ShapeDtyp...  21.8 us
    unnamed x1, local copies, waits for them, and re-layouts  2.18 us

profile of v2, /device:TPU:0, one launch (start us, length us, event | category | flops | bytes accessed | tf_op | source)
XLA Modules:
  0.0 24.0 jit_solution(13782849039287342867)
XLA Ops:
  0.0 21.8 %shard_map.46 = f32[2,7,128,128]{3,2,1,0:T(8,128)} custom-call(f32[2,7,128,128]{3,2,1,0:T(8,128)} %prev.1, f32[2,4,128,128]{3,2,1,0:T(8,128)} %diss.1, s32[4,128,128]{2,1,0:T(8,128)} %mat.1, s32[3,128,128]{2,1,0:T(8,128)} %cool.1), custom_call_target="tpu_custom_call" | custom-call | tf_op jit(solution)/shard_map/pallas_call | solution.py:416
  21.8 2.2 %copy.6 = f32[2,7,128,128]{3,2,1,0:T(8,128)} copy(f32[2,7,128,128]{3,2,1,0:T(8,128)} %shard_map.46) | data formatting | bytes 1835008
